TPU v7x, 256 devices: a 8x8x2 block of a 8x8x16 slice. The times are simulated.
256 devices in a mesh: scene: 2 (over z), view: 128 (over y, x, core).
Axes of the slice: x: 8, y: 8, z: 2, core: 2. Of those that a mesh axis runs over, the one named last changes fastest.
The devices are a block of a 8x8x16 slice.
Arguments:
- latents: bfloat16 [2048, 64, 512], P(('scene', 'view')), parts along dimension 0, may hold values from -48 to 48
- norm_gain: float32 [512], replicated, may hold values from 0.1 to 1.9
- norm_shift: float32 [512], replicated, may hold values from -3 to 3
- w_first: bfloat16 [512, 3, 3, 512], replicated, may hold values from -0.09375 to 0.09375
- bias_first: float32 [512], replicated, may hold values from -3 to 3
- w_second: bfloat16 [512, 3, 3, 512], replicated, may hold values from -0.09375 to 0.09375
- bias_second: float32 [512], replicated, may hold values from -3 to 3
Outputs:
- decoded: bfloat16 [4096, 128, 512], P(('scene', 'view')), parts along dimension 0
There are 2 independent parts, one for each index of `scene`. A program takes and returns all parts, laid end to end along the dimension named above; an argument that names none is the same for every part. Nothing has to cross between parts.
All inputs are finite; a program needn't handle non-finite values.
Results may differ from a plain program's by a relative error of at most 0.0051.
Values may be sent and summed in bfloat16 or wider, within the bound.
A program may use at most 128 MiB of HBM per device.

v0:
```python
import jax
import jax.numpy as jnp
from jax import lax
from jax.sharding import Mesh
from jax.sharding import PartitionSpec as P

GROUPS = 32
H_LAT = 32
VIEW = ("view_0", "view_1", "view_2")
SCENE_VIEW = ("scene", "view_0", "view_1", "view_2")
epsilon = 1e-06


def one_axis_at_a_time(array, axes):
    for axis in axes:
        array = lax.psum(array, axis)
    return array


def shifted(block, axis, distance):
    devices = range(lax.axis_size(axis))
    route = [(i - distance, i) for i in devices if i - distance in devices]
    return lax.ppermute(block, axis, route)


def conv_taps(padded, filters, out_rows, out_cols):
    result = None
    for tap_row in range(3):
        for tap_col in range(3):
            window = padded[tap_row : tap_row + out_rows, tap_col : tap_col + out_cols, :]
            term = jnp.einsum(
                "rwi,oi->rwo",
                window,
                filters[:, tap_row, tap_col, :],
                preferred_element_type=jnp.float32,
            )
            result = term if result is None else result + term
    return result


def pad_columns(block):
    return jnp.pad(block, ((0, 0), (1, 1), (0, 0)))


def keep_inside(block, first_row):
    position = first_row + jnp.arange(block.shape[0], dtype=jnp.int32)
    inside = (position >= 0) & (position < H_LAT)
    return jnp.where(inside[:, None, None], block, jnp.zeros((), block.dtype))


def spread_channels(group_values, channels):
    return jnp.broadcast_to(group_values[:, None], (GROUPS, channels // GROUPS)).reshape(channels)


def group_total(channel_values, channels):
    return jnp.sum(channel_values.reshape(GROUPS, channels // GROUPS), axis=1)


def per_device(latents, norm_gain, norm_shift, w_first, bias_first, w_second, bias_second):
    slab_rows, columns, channels = latents.shape
    slab_count = H_LAT // slab_rows
    view_count = lax.axis_size(VIEW) // slab_count
    slab_index = lax.axis_index(VIEW) // view_count
    slab_start = slab_index * slab_rows
    entries = float(slab_rows * columns * (channels // GROUPS) * lax.axis_size(VIEW))
    values = latents.astype(jnp.float32)
    group_sums = group_total(jnp.sum(values, axis=(0, 1)), channels)
    group_squares = group_total(jnp.sum(values * values, axis=(0, 1)), channels)
    total_sums, total_squares = (
        one_axis_at_a_time(group_sums, VIEW),
        one_axis_at_a_time(group_squares, VIEW),
    )
    group_mean = total_sums / entries
    group_var = total_squares / entries - group_mean * group_mean
    channel_scale = spread_channels(lax.rsqrt(group_var + epsilon), channels) * norm_gain
    channel_offset = norm_shift - spread_channels(group_mean, channels) * channel_scale
    above = shifted(latents[-2:], VIEW, view_count)
    below = shifted(latents[:2], VIEW, -view_count)
    deeper = jnp.concatenate([above, latents, below], axis=0)
    active = keep_inside(
        jax.nn.silu(deeper.astype(jnp.float32) * channel_scale + channel_offset).astype(
            jnp.bfloat16
        ),
        slab_start - 2,
    )
    filtered = conv_taps(pad_columns(active), w_first, slab_rows + 2, columns)
    mixed = (deeper[1:-1].astype(jnp.float32) + filtered + bias_first).astype(jnp.bfloat16)
    mixed = keep_inside(mixed, slab_start - 1)
    tall_rows = mixed.shape[0]
    doubled = jnp.broadcast_to(mixed[:, None, :, None, :], (tall_rows, 2, columns, 2, channels))
    doubled = doubled.reshape(2 * tall_rows, 2 * columns, channels)
    doubled = doubled[1 : 2 * slab_rows + 3]
    decoded = conv_taps(pad_columns(doubled), w_second, 2 * slab_rows, 2 * columns) + bias_second
    return decoded.astype(jnp.bfloat16)


def solution(mesh):
    torus = Mesh(
        mesh.devices.reshape(mesh.shape["scene"], 8, 8, 2), ("scene", "view_0", "view_1", "view_2")
    )
    in_specs = (P(SCENE_VIEW, None, None), P(), P(), P(), P(), P(), P())
    out_specs = P(SCENE_VIEW, None, None)
    return jax.shard_map(
        per_device, mesh=torus, in_specs=in_specs, out_specs=out_specs, check_vma=False
    )
```

profile of v0, /device:TPU:513, one launch (start us, length us, event | category | flops | bytes accessed | tf_op | source)
XLA Modules:
  0.0 123.4 jit_solution(8595949860446383407)
XLA Ops:
  0.0 1.0 fusion.96
  1.0 1.3 %collective-permute-start.1 = (bf16[2,64,512]{2,1,0:T(8,128)(2,1)S(1)}, bf16[2,64,512]{2,1,0:T(8,128)(2,1)S(1)}, u32[]{:S(2)}, u32[]{:S(2)}) collective-permute-start(bf16[2,64,512]{2,1,0:T(8,128)(2,1)S(1)} %get-tuple-element.15), channel_id=1, source_target_pairs={{32,0},{33,1},{34,2},{35,3},{36,4},{37,5},{38,6},{39,7},{40,8},{41... | collective-permute-start | bytes 393224 | tf_op jit(solution)/shard_map/ppermute | solution.py:23
  2.3 8.1 %collective-permute-start = (bf16[2,64,512]{2,1,0:T(8,128)(2,1)S(1)}, bf16[2,64,512]{2,1,0:T(8,128)(2,1)S(1)}, u32[]{:S(2)}, u32[]{:S(2)}) collective-permute-start(bf16[2,64,512]{2,1,0:T(8,128)(2,1)S(1)} %get-tuple-element.16), channel_id=1, source_target_pairs={{0,32},{1,33},{2,34},{3,35},{4,36},{5,37},{6,38},{7,39},{8,40},{9,... | collective-permute-start | bytes 393224 | tf_op jit(solution)/shard_map/ppermute | solution.py:23
  10.4 1.2 fusion.23
  11.7 0.1 reshape.37
  11.7 0.1 reshape.38
  11.8 0.1 reduce_sum.37
  11.9 0.1 reduce_sum.39
  12.1 17.7 %all-reduce.3 = (f32[32]{0:T(128)S(1)}, f32[32]{0:T(128)S(1)}) all-reduce(f32[32]{0:T(128)S(1)} %reduce_sum.39, f32[32]{0:T(128)S(1)} %reduce_sum.37), channel_id=1, replica_groups=mesh['scene'=2,'view_0'=8,'view_1'=8,'view_2'=2] {'view_0'}, use_global_device_ids=true, to_apply=%region_7.8 | all-reduce | flops 64 | bytes 512 | tf_op jit(solution)/shard_map/psum | solution.py:16
  29.8 14.1 %all-reduce.2 = (f32[32]{0:T(128)S(1)}, f32[32]{0:T(128)S(1)}) all-reduce(f32[32]{0:T(128)S(1)} %get-tuple-element.9, f32[32]{0:T(128)S(1)} %get-tuple-element.10), channel_id=1, replica_groups=mesh['scene'=2,'view_0'=8,'view_1'=8,'view_2'=2] {'view_1'}, use_global_device_ids=true, to_apply=%region_8.9 | all-reduce | flops 64 | bytes 512 | tf_op jit(solution)/shard_map/psum | solution.py:16
  43.9 16.6 %all-reduce.4 = (f32[32]{0:T(128)S(1)}, f32[32]{0:T(128)S(1)}) all-reduce(f32[32]{0:T(128)S(1)} %get-tuple-element.7, f32[32]{0:T(128)S(1)} %get-tuple-element.8), channel_id=1, replica_groups=mesh['scene'=2,'view_0'=8,'view_1'=8,'view_2'=2] {'view_2'}, use_global_device_ids=true, to_apply=%region_9.10 | all-reduce | flops 64 | bytes 512 | tf_op jit(solution)/shard_map/psum | solution.py:16
  60.5 0.1 broadcast_in_dim.52
  60.6 0.1 reshape.39
  60.6 0.1 broadcast_in_dim.53
  60.7 0.1 reshape.40
  60.8 0.7 multiply_subtract_fusion
  61.5 0.0 collective-permute-done
  61.6 0.0 copy-start.2
  61.6 1.2 constant_dynamic-update-slice_fusion.1
  62.8 0.0 collective-permute-done.1
  62.8 0.5 fusion.24
  63.4 1.6 %fusion.34 = f32[10,64,512]{2,1,0:T(8,128)S(1)} fusion(bf16[12,64,512]{2,1,0:T(8,128)(2,1)S(1)} %fusion.24, bf16[512,3,3,512]{3,0,2,1:T(8,128)(2,1)} %param.10), kind=kOutput, calls=%fused_computation.42 | convolution fusion | flops 335544320 | bytes 2621440 | tf_op jit(solution)/shard_map/rwi,oi->rwo/dot_general | solution.py:31
  64.9 0.0 copy-done.2
  65.0 0.5 fusion.32
  65.5 0.5 fusion.30
  66.1 0.5 fusion.28
  66.6 0.5 fusion.26
  67.1 0.5 fusion.36
  67.7 0.5 fusion.16
  68.2 0.0 copy-start.3
  68.3 0.5 fusion.14
  68.8 0.1 copy-done.3
  68.9 0.7 fusion.25
  69.6 0.0 copy-start.1
  69.6 3.5 %broadcast_in_dim.56 = bf16[10,2,64,2,512]{4,3,2,1,0:T(2,128)(2,1)} broadcast(bf16[10,64,512]{2,1,0:T(8,128)(2,1)S(1)} %fusion.25), dimensions={0,2,4} | broadcast | bytes 3276800 | tf_op jit(solution)/shard_map/broadcast_in_dim | solution.py:90
  73.1 3.8 %reshape.41 = bf16[20,128,512]{2,1,0:T(8,128)(2,1)S(1)} reshape(bf16[10,2,64,2,512]{4,3,2,1,0:T(2,128)(2,1)} %broadcast_in_dim.56) | data formatting | bytes 5242880 | tf_op jit(solution)/shard_map/reshape | solution.py:91
  76.9 0.0 copy-done.1
  76.9 0.0 slice-start.1
  76.9 0.2 slice.175
  77.1 0.0 slice-start.2
  77.1 4.4 %fusion.8 = f32[16,128,512]{2,1,0:T(8,128)} fusion(bf16[18,128,512]{2,1,0:T(8,128)(2,1)S(1)} %slice.175, bf16[512,3,3,512]{3,0,2,1:T(8,128)(2,1)} %param.12), kind=kOutput, calls=%fused_computation.9 | convolution fusion | flops 1073741824 | bytes 7077888 | tf_op jit(solution)/shard_map/rwi,oi->rwo/dot_general | solution.py:31
  81.5 4.3 %fusion.6 = f32[16,128,512]{2,1,0:T(8,128)} fusion(bf16[18,128,512]{2,1,0:T(8,128)(2,1)S(1)} %slice.175, bf16[512,3,3,512]{3,0,2,1:T(8,128)(2,1)} %param.12), kind=kOutput, calls=%fused_computation.7 | convolution fusion | flops 1073741824 | bytes 7077888 | tf_op jit(solution)/shard_map/rwi,oi->rwo/dot_general | solution.py:31
  85.8 0.0 slice-done.1
  85.8 0.0 slice-done.2
  85.8 3.3 %fusion.4 = f32[16,128,512]{2,1,0:T(8,128)} fusion(bf16[18,128,512]{2,1,0:T(8,128)(2,1)S(1)} %slice.175, bf16[512,3,3,512]{3,0,2,1:T(8,128)(2,1)S(1)} %bitcast.99), kind=kOutput, calls=%fused_computation.5 | convolution fusion | flops 1073741824 | bytes 7077888 | tf_op jit(solution)/shard_map/rwi,oi->rwo/dot_general | solution.py:31
  89.1 3.3 %fusion.2 = f32[16,128,512]{2,1,0:T(8,128)} fusion(bf16[18,128,512]{2,1,0:T(8,128)(2,1)S(1)} %slice.175, bf16[512,3,3,512]{3,0,2,1:T(8,128)(2,1)S(1)} %bitcast.99), kind=kOutput, calls=%fused_computation.3 | convolution fusion | flops 1073741824 | bytes 7077888 | tf_op jit(solution)/shard_map/rwi,oi->rwo/dot_general | solution.py:31
  92.4 3.2 %fusion = f32[16,128,512]{2,1,0:T(8,128)} fusion(bf16[18,128,512]{2,1,0:T(8,128)(2,1)S(1)} %slice.175, bf16[512,3,3,512]{3,0,2,1:T(8,128)(2,1)S(1)} %bitcast.99), kind=kOutput, calls=%fused_computation.1 | convolution fusion | flops 1073741824 | bytes 7077888 | tf_op jit(solution)/shard_map/rwi,oi->rwo/dot_general | solution.py:31
  95.6 3.3 %fusion.10 = f32[16,128,512]{2,1,0:T(8,128)} fusion(bf16[18,128,512]{2,1,0:T(8,128)(2,1)S(1)} %slice.175, bf16[512,3,3,512]{3,0,2,1:T(8,128)(2,1)S(1)} %bitcast.99), kind=kOutput, calls=%fused_computation.11 | convolution fusion | flops 1073741824 | bytes 7077888 | tf_op jit(solution)/shard_map/rwi,oi->rwo/dot_general | solution.py:31
  98.9 0.0 slice-start
  98.9 3.3 %fusion.52 = f32[16,128,512]{2,1,0:T(8,128)} fusion(bf16[20,128,512]{2,1,0:T(8,128)(2,1)S(1)} %reshape.41, bf16[512,3,3,512]{3,0,2,1:T(8,128)(2,1)S(1)} %bitcast.99), kind=kOutput, calls=%fused_computation.60 | convolution fusion | flops 1073741824 | bytes 7340032 | tf_op jit(solution)/shard_map/rwi,oi->rwo/dot_general | solution.py:31
  102.2 0.0 slice-done
  102.2 2.9 %broadcast_in_dim.57 = bf16[8,2,64,2,512]{4,3,2,1,0:T(2,128)(2,1)} broadcast(bf16[8,64,512]{2,1,0:T(8,128)(2,1)S(1)} %slice-done), dimensions={0,2,4} | broadcast | bytes 2621440 | tf_op jit(solution)/shard_map/broadcast_in_dim | solution.py:90
  105.1 4.1 %slice.164 = bf16[16,128,512]{2,1,0:T(8,128)(2,1)} reshape(bf16[8,2,64,2,512]{4,3,2,1,0:T(2,128)(2,1)} %broadcast_in_dim.57) | data formatting | bytes 4194304 | tf_op jit(solution)/shard_map/slice | solution.py:30
  109.3 0.0 copy-start
  109.3 0.0 copy-start.4
  109.3 3.1 %fusion.48 = f32[16,128,512]{2,1,0:T(8,128)S(1)} fusion(bf16[16,128,512]{2,1,0:T(8,128)(2,1)} %slice.164, bf16[512,3,3,512]{3,0,2,1:T(8,128)(2,1)} %param.12), kind=kOutput, calls=%fused_computation.56 | convolution fusion | flops 1073741824 | bytes 6815744 | tf_op jit(solution)/shard_map/rwi,oi->rwo/dot_general | solution.py:31
  112.4 0.0 copy-done
  112.4 0.0 copy-done.4
  112.4 11.0 %add_convert_fusion = bf16[16,128,512]{2,1,0:T(8,128)(2,1)} fusion(f32[16,128,512]{2,1,0:T(8,128)} %fusion, f32[16,128,512]{2,1,0:T(8,128)} %fusion.2, f32[16,128,512]{2,1,0:T(8,128)} %fusion.4, f32[16,128,512]{2,1,0:T(8,128)S(1)} %fusion.48, f32[16,128,512]{2,1,0:T(8,128)} %fusion.6, f32[16,128,512]{2,1,0:T(8,128)S(1)} %copy-done, ...), kind=kOutput, calls=%fused_computation | convolution fusion | flops 1084227584 | bytes 38799360 | tf_op jit(solution)/shard_map/rwi,oi->rwo/dot_general | solution.py:31
  (6 shorter events, 0.0 us)
Async XLA Ops:
  1.0 61.8 %collective-permute-start.1 = (bf16[2,64,512]{2,1,0:T(8,128)(2,1)S(1)}, bf16[2,64,512]{2,1,0:T(8,128)(2,1)S(1)}, u32[]{:S(2)}, u32[]{:S(2)}) collective-permute-start(bf16[2,64,512]{2,1,0:T(8,128)(2,1)S(1)} %get-tuple-element.15), channel_id=1, source_target_pairs={{32,0},{33,1},{34,2},{35,3},{36,4},{37,5},{38,6},{39,7},{40,8},{41... | collective-permute-start | bytes 393224 | tf_op jit(solution)/shard_map/ppermute | solution.py:23
  2.3 59.2 %collective-permute-start = (bf16[2,64,512]{2,1,0:T(8,128)(2,1)S(1)}, bf16[2,64,512]{2,1,0:T(8,128)(2,1)S(1)}, u32[]{:S(2)}, u32[]{:S(2)}) collective-permute-start(bf16[2,64,512]{2,1,0:T(8,128)(2,1)S(1)} %get-tuple-element.16), channel_id=1, source_target_pairs={{0,32},{1,33},{2,34},{3,35},{4,36},{5,37},{6,38},{7,39},{8,40},{9,... | collective-permute-start | bytes 393224 | tf_op jit(solution)/shard_map/ppermute | solution.py:23
  61.6 3.4 %copy-start.2 = (bf16[512,3,3,512]{3,0,2,1:T(8,128)(2,1)S(1)}, bf16[512,3,3,512]{3,0,2,1:T(8,128)(2,1)}, u32[]{:S(2)}) copy-start(bf16[512,3,3,512]{3,0,2,1:T(8,128)(2,1)} %param.10) | copy-start | bytes 14155780
  68.2 0.7 copy-start.3
  69.6 7.3 %copy-start.1 = (bf16[10,64,512]{2,1,0:T(8,128)(2,1)}, bf16[10,64,512]{2,1,0:T(8,128)(2,1)S(1)}, u32[]{:S(2)}) copy-start(bf16[10,64,512]{2,1,0:T(8,128)(2,1)S(1)} %fusion.25) | copy-start | bytes 1966084
  76.9 8.9 %slice-start.1 = ((s8[4718592]{0:T(1024)(128)(4,1)}), s8[4194304]{0:T(1024)(128)(4,1)S(1)}, s32[]{:S(2)}) async-start(s8[4718592]{0:T(1024)(128)(4,1)} %bitcast.98), calls=%async_computation.1 | async-start | bytes 8388608
  77.1 8.8 %slice-start.2 = ((s8[4718592]{0:T(1024)(128)(4,1)}), s8[524288]{0:T(1024)(128)(4,1)S(1)}, s32[]{:S(2)}) async-start(s8[4718592]{0:T(1024)(128)(4,1)} %bitcast.98), calls=%async_computation.2 | async-start | bytes 1048576
  98.9 3.3 %slice-start = ((bf16[10,64,512]{2,1,0:T(8,128)(2,1)}), bf16[8,64,512]{2,1,0:T(8,128)(2,1)S(1)}, s32[]{:S(2)}) async-start(bf16[10,64,512]{2,1,0:T(8,128)(2,1)} %copy-done.1), calls=%async_computation | async-start | bytes 1048576 | tf_op jit(solution)/shard_map/slice | solution.py:30
  109.3 3.1 %copy-start = (f32[16,128,512]{2,1,0:T(8,128)S(1)}, f32[16,128,512]{2,1,0:T(8,128)}, u32[]{:S(2)}) copy-start(f32[16,128,512]{2,1,0:T(8,128)} %fusion.8) | copy-start | bytes 12582916
  109.3 3.1 %copy-start.4 = (f32[512]{0:T(512)S(1)}, f32[512]{0:T(512)}, u32[]{:S(2)}) copy-start(f32[512]{0:T(512)} %param.13) | copy-start | bytes 6148
where the time goes:
time: 124 us; the launch traced here: 123 us
  blocking collectives  48.4 us (39%)
  matrix products  45.2 us (36%)
  local copies, waits for them, and re-layouts  17.3 us (14%)
  starting transfers between devices  9.42 us (8%)
  other arithmetic  2.69 us (2%)
    psum x3, blocking collectives, one_axis_at_a_time(): array = lax.psum(array, axis)  48.4 us
    dot_general x18, matrix products, conv_taps(): jnp.einsum('rwi,oi->rwo', window, filters[:, tap_row, tap_col, :], prefer...  45.2 us
    ppermute x2, starting transfers between devices, shifted(): return lax.ppermute(block, axis, route)  9.42 us
    broadcast_in_dim x2, local copies, waits for them, and re-layouts, per_device(): jnp.broadcast_to(mixed[:, None, :, None, :], (tall_rows, 2, columns, 2, c...  6.44 us
    slice x3, local copies, waits for them, and re-layouts, conv_taps(): window = padded[tap_row:tap_row + out_rows, tap_col:tap_col + out_cols, :]  4.14 us
    reshape x1, local copies, waits for them, and re-layouts, per_device(): doubled = doubled.reshape(2 * tall_rows, 2 * columns, channels)  3.75 us
  transfers between devices with their start and end apart: 2, of which 0 were waited for; matrix products, arithmetic and copies ran while one was open for 3% of the time, Pallas kernels for 0%

commit v1 on v0

--- a/solution.py
+++ b/solution.py
@@ -13,7 +13,7 @@
 
 def one_axis_at_a_time(array, axes):
     for axis in axes:
-        array = lax.psum(array, axis)
+        array = jnp.sum(lax.all_gather(array, axis), axis=0)
     return array
 
 

time: 124 us -> 132 us (1.065)
  local copies, waits for them, and re-layouts: 17.3 us -> 23 us
  between operations: 0.26 us -> 2.17 us
    psum x3 -> x0, blocking collectives: 48.4 us -> none  [one_axis_at_a_time(): array = lax.psum(array, axis)]
    unnamed x0 -> x3, blocking collectives: none -> 48.3 us
    unnamed x16 -> x31, local copies, waits for them, and re-layouts: 1.4 us -> 6.54 us
  transfers between devices with their start and end apart: 2 -> 2, of which waited for: 0 -> 0; matrix products, arithmetic and copies ran while one was open for 3% -> 7% of each run, Pallas kernels for 0% -> 0%
where the time goes in v1:
time: 132 us; the launch traced here: 131 us
  blocking collectives  48.3 us (37%)
  matrix products  45.2 us (34%)
  local copies, waits for them, and re-layouts  23 us (17%)
  starting transfers between devices  9.42 us (7%)
  other arithmetic  2.81 us (2%)
  between operations  2.17 us (2%)
    unnamed x3, blocking collectives  48.3 us
    dot_general x18, matrix products, conv_taps(): jnp.einsum('rwi,oi->rwo', window, filters[:, tap_row, tap_col, :], prefer...  45.2 us
    ppermute x2, starting transfers between devices, shifted(): return lax.ppermute(block, axis, route)  9.42 us
    unnamed x31, local copies, waits for them, and re-layouts  6.54 us
    broadcast_in_dim x2, local copies, waits for them, and re-layouts, per_device(): jnp.broadcast_to(mixed[:, None, :, None, :], (tall_rows, 2, columns, 2, c...  6.44 us
    slice x3, local copies, waits for them, and re-layouts, conv_taps(): window = padded[tap_row:tap_row + out_rows, tap_col:tap_col + out_cols, :]  4.14 us
    reshape x1, local copies, waits for them, and re-layouts, per_device(): doubled = doubled.reshape(2 * tall_rows, 2 * columns, channels)  3.75 us
  transfers between devices with their start and end apart: 2, of which 0 were waited for; matrix products, arithmetic and copies ran while one was open for 7% of the time, Pallas kernels for 0%

profile of v1, /device:TPU:513, one launch (start us, length us, event | category | flops | bytes accessed | tf_op | source)
XLA Modules:
  0.0 130.9 jit_solution(5807273469263583007)
XLA Ops:
  0.0 1.0 fusion.96
  1.0 1.3 collective-permute-start.1
  2.3 8.1 %collective-permute-start = (bf16[2,64,512]{2,1,0:T(8,128)(2,1)S(1)}, bf16[2,64,512]{2,1,0:T(8,128)(2,1)S(1)}, u32[]{:S(2)}, u32[]{:S(2)}) collective-permute-start(bf16[2,64,512]{2,1,0:T(8,128)(2,1)S(1)} %get-tuple-element.16), channel_id=1, source_target_pairs={{0,32},{1,33},{2,34},{3,35},{4,36},{5,37},{6,38},{7,39},{8,40},{9,... | collective-permute-start | bytes 393224 | tf_op jit(solution)/shard_map/ppermute | solution.py:23
  10.4 1.2 fusion.23
  11.7 1.3 dynamic-slice.2
  12.9 1.3 dynamic-slice.1
  15.4 1.3 dynamic-slice
  17.3 0.1 reshape.47
  17.4 0.1 reshape.48
  17.5 0.1 reduce_sum.91
  17.6 0.1 reduce_sum.96
  17.7 0.2 dynamic-update-slice
  18.0 0.2 dynamic-update-slice.3
  18.2 17.0 %all-reduce.9 = (f32[256]{0:T(256)S(1)}, f32[256]{0:T(256)S(1)}) all-reduce(f32[256]{0:T(256)S(1)} %dynamic-update-slice.3, f32[256]{0:T(256)S(1)} %dynamic-update-slice), channel_id=5, replica_groups=mesh['scene'=2,'view_0'=8,'view_1'=8,'view_2'=2] {'view_0'}, use_global_device_ids=true, to_apply=%add.5 | all-reduce | flops 512 | bytes 4096
  35.1 0.1 reshape.55
  35.2 0.1 reshape.52
  35.3 0.2 dynamic-update-slice.4
  35.6 0.2 dynamic-update-slice.1
  35.8 14.2 %all-reduce.8 = (f32[256]{0:T(256)S(1)}, f32[256]{0:T(256)S(1)}) all-reduce(f32[256]{0:T(256)S(1)} %dynamic-update-slice.4, f32[256]{0:T(256)S(1)} %dynamic-update-slice.1), channel_id=6, replica_groups=mesh['scene'=2,'view_0'=8,'view_1'=8,'view_2'=2] {'view_1'}, use_global_device_ids=true, to_apply=%add.6 | all-reduce | flops 512 | bytes 4096
  50.0 0.1 reshape.56
  50.1 0.1 reshape.53
  50.2 0.2 dynamic-update-slice.5
  50.5 0.2 dynamic-update-slice.2
  50.7 17.2 %all-reduce.10 = (f32[64]{0:T(128)S(1)}, f32[64]{0:T(128)S(1)}) all-reduce(f32[64]{0:T(128)S(1)} %dynamic-update-slice.5, f32[64]{0:T(128)S(1)} %dynamic-update-slice.2), channel_id=7, replica_groups=mesh['scene'=2,'view_0'=8,'view_1'=8,'view_2'=2] {'view_2'}, use_global_device_ids=true, to_apply=%add.7 | all-reduce | flops 128 | bytes 1024
  67.8 0.1 reshape.57
  67.9 0.1 reshape.54
  68.0 0.1 broadcast_in_dim.52
  68.1 0.1 reshape.49
  68.2 0.1 broadcast_in_dim.53
  68.3 0.1 reshape.50
  68.3 0.7 multiply_subtract_fusion
  69.1 0.0 collective-permute-done
  69.1 0.0 copy-start.2
  69.1 1.2 constant_dynamic-update-slice_fusion.1
  70.4 0.0 collective-permute-done.1
  70.4 0.5 fusion.24
  70.9 1.6 %fusion.34 = f32[10,64,512]{2,1,0:T(8,128)S(1)} fusion(bf16[12,64,512]{2,1,0:T(8,128)(2,1)S(1)} %fusion.24, bf16[512,3,3,512]{3,0,2,1:T(8,128)(2,1)} %param.10), kind=kOutput, calls=%fused_computation.42 | convolution fusion | flops 335544320 | bytes 2621440 | tf_op jit(solution)/shard_map/rwi,oi->rwo/dot_general | solution.py:31
  72.5 0.5 fusion.32
  73.1 0.5 fusion.30
  73.6 0.5 fusion.28
  74.1 0.5 fusion.26
  74.7 0.5 fusion.36
  75.2 0.5 fusion.16
  75.8 0.0 copy-start.3
  75.8 0.5 fusion.14
  76.4 0.1 copy-done.3
  76.5 0.7 fusion.25
  77.2 0.0 copy-start.1
  77.2 3.5 %broadcast_in_dim.56 = bf16[10,2,64,2,512]{4,3,2,1,0:T(2,128)(2,1)} broadcast(bf16[10,64,512]{2,1,0:T(8,128)(2,1)S(1)} %fusion.25), dimensions={0,2,4} | broadcast | bytes 3276800 | tf_op jit(solution)/shard_map/broadcast_in_dim | solution.py:90
  80.7 3.8 %reshape.51 = bf16[20,128,512]{2,1,0:T(8,128)(2,1)S(1)} reshape(bf16[10,2,64,2,512]{4,3,2,1,0:T(2,128)(2,1)} %broadcast_in_dim.56) | data formatting | bytes 5242880 | tf_op jit(solution)/shard_map/reshape | solution.py:91
  84.4 0.0 slice-start.1
  84.5 0.2 slice.175
  84.6 0.0 slice-start.2
  84.6 4.4 %fusion.8 = f32[16,128,512]{2,1,0:T(8,128)} fusion(bf16[18,128,512]{2,1,0:T(8,128)(2,1)S(1)} %slice.175, bf16[512,3,3,512]{3,0,2,1:T(8,128)(2,1)} %param.12), kind=kOutput, calls=%fused_computation.9 | convolution fusion | flops 1073741824 | bytes 7077888 | tf_op jit(solution)/shard_map/rwi,oi->rwo/dot_general | solution.py:31
  89.0 4.3 %fusion.6 = f32[16,128,512]{2,1,0:T(8,128)} fusion(bf16[18,128,512]{2,1,0:T(8,128)(2,1)S(1)} %slice.175, bf16[512,3,3,512]{3,0,2,1:T(8,128)(2,1)} %param.12), kind=kOutput, calls=%fused_computation.7 | convolution fusion | flops 1073741824 | bytes 7077888 | tf_op jit(solution)/shard_map/rwi,oi->rwo/dot_general | solution.py:31
  93.4 3.3 %fusion.4 = f32[16,128,512]{2,1,0:T(8,128)} fusion(bf16[18,128,512]{2,1,0:T(8,128)(2,1)S(1)} %slice.175, bf16[512,3,3,512]{3,0,2,1:T(8,128)(2,1)S(1)} %bitcast.102), kind=kOutput, calls=%fused_computation.5 | convolution fusion | flops 1073741824 | bytes 7077888 | tf_op jit(solution)/shard_map/rwi,oi->rwo/dot_general | solution.py:31
  96.7 3.3 %fusion.2 = f32[16,128,512]{2,1,0:T(8,128)} fusion(bf16[18,128,512]{2,1,0:T(8,128)(2,1)S(1)} %slice.175, bf16[512,3,3,512]{3,0,2,1:T(8,128)(2,1)S(1)} %bitcast.102), kind=kOutput, calls=%fused_computation.3 | convolution fusion | flops 1073741824 | bytes 7077888 | tf_op jit(solution)/shard_map/rwi,oi->rwo/dot_general | solution.py:31
  99.9 3.2 %fusion = f32[16,128,512]{2,1,0:T(8,128)} fusion(bf16[18,128,512]{2,1,0:T(8,128)(2,1)S(1)} %slice.175, bf16[512,3,3,512]{3,0,2,1:T(8,128)(2,1)S(1)} %bitcast.102), kind=kOutput, calls=%fused_computation.1 | convolution fusion | flops 1073741824 | bytes 7077888 | tf_op jit(solution)/shard_map/rwi,oi->rwo/dot_general | solution.py:31
  103.2 3.3 %fusion.10 = f32[16,128,512]{2,1,0:T(8,128)} fusion(bf16[18,128,512]{2,1,0:T(8,128)(2,1)S(1)} %slice.175, bf16[512,3,3,512]{3,0,2,1:T(8,128)(2,1)S(1)} %bitcast.102), kind=kOutput, calls=%fused_computation.11 | convolution fusion | flops 1073741824 | bytes 7077888 | tf_op jit(solution)/shard_map/rwi,oi->rwo/dot_general | solution.py:31
  106.5 3.3 %fusion.52 = f32[16,128,512]{2,1,0:T(8,128)} fusion(bf16[20,128,512]{2,1,0:T(8,128)(2,1)S(1)} %reshape.51, bf16[512,3,3,512]{3,0,2,1:T(8,128)(2,1)S(1)} %bitcast.102), kind=kOutput, calls=%fused_computation.60 | convolution fusion | flops 1073741824 | bytes 7340032 | tf_op jit(solution)/shard_map/rwi,oi->rwo/dot_general | solution.py:31
  109.7 2.9 %broadcast_in_dim.57 = bf16[8,2,64,2,512]{4,3,2,1,0:T(2,128)(2,1)} broadcast(bf16[8,64,512]{2,1,0:T(8,128)(2,1)S(1)} %slice-done), dimensions={0,2,4} | broadcast | bytes 2621440 | tf_op jit(solution)/shard_map/broadcast_in_dim | solution.py:90
  112.7 4.1 %slice.164 = bf16[16,128,512]{2,1,0:T(8,128)(2,1)} reshape(bf16[8,2,64,2,512]{4,3,2,1,0:T(2,128)(2,1)} %broadcast_in_dim.57) | data formatting | bytes 4194304 | tf_op jit(solution)/shard_map/slice | solution.py:30
  116.8 3.1 %fusion.48 = f32[16,128,512]{2,1,0:T(8,128)S(1)} fusion(bf16[16,128,512]{2,1,0:T(8,128)(2,1)} %slice.164, bf16[512,3,3,512]{3,0,2,1:T(8,128)(2,1)} %param.12), kind=kOutput, calls=%fused_computation.56 | convolution fusion | flops 1073741824 | bytes 6815744 | tf_op jit(solution)/shard_map/rwi,oi->rwo/dot_general | solution.py:31
  119.9 11.0 %add_convert_fusion = bf16[16,128,512]{2,1,0:T(8,128)(2,1)} fusion(f32[16,128,512]{2,1,0:T(8,128)} %fusion, f32[16,128,512]{2,1,0:T(8,128)} %fusion.2, f32[16,128,512]{2,1,0:T(8,128)} %fusion.4, f32[16,128,512]{2,1,0:T(8,128)S(1)} %fusion.48, f32[16,128,512]{2,1,0:T(8,128)} %fusion.6, f32[16,128,512]{2,1,0:T(8,128)S(1)} %copy-done, ...), kind=kOutput, calls=%fused_computation | convolution fusion | flops 1084227584 | bytes 38799360 | tf_op jit(solution)/shard_map/rwi,oi->rwo/dot_general | solution.py:31
  (28 shorter events, 0.2 us)
Async XLA Ops:
  1.0 69.4 %collective-permute-start.1 = (bf16[2,64,512]{2,1,0:T(8,128)(2,1)S(1)}, bf16[2,64,512]{2,1,0:T(8,128)(2,1)S(1)}, u32[]{:S(2)}, u32[]{:S(2)}) collective-permute-start(bf16[2,64,512]{2,1,0:T(8,128)(2,1)S(1)} %get-tuple-element.15), channel_id=1, source_target_pairs={{32,0},{33,1},{34,2},{35,3},{36,4},{37,5},{38,6},{39,7},{40,8},{41... | collective-permute-start | bytes 393224 | tf_op jit(solution)/shard_map/ppermute | solution.py:23
  2.3 66.8 %collective-permute-start = (bf16[2,64,512]{2,1,0:T(8,128)(2,1)S(1)}, bf16[2,64,512]{2,1,0:T(8,128)(2,1)S(1)}, u32[]{:S(2)}, u32[]{:S(2)}) collective-permute-start(bf16[2,64,512]{2,1,0:T(8,128)(2,1)S(1)} %get-tuple-element.16), channel_id=1, source_target_pairs={{0,32},{1,33},{2,34},{3,35},{4,36},{5,37},{6,38},{7,39},{8,40},{9,... | collective-permute-start | bytes 393224 | tf_op jit(solution)/shard_map/ppermute | solution.py:23
  69.1 3.4 %copy-start.2 = (bf16[512,3,3,512]{3,0,2,1:T(8,128)(2,1)S(1)}, bf16[512,3,3,512]{3,0,2,1:T(8,128)(2,1)}, u32[]{:S(2)}) copy-start(bf16[512,3,3,512]{3,0,2,1:T(8,128)(2,1)} %param.10) | copy-start | bytes 14155780
  75.8 0.7 copy-start.3
  77.2 7.3 %copy-start.1 = (bf16[10,64,512]{2,1,0:T(8,128)(2,1)}, bf16[10,64,512]{2,1,0:T(8,128)(2,1)S(1)}, u32[]{:S(2)}) copy-start(bf16[10,64,512]{2,1,0:T(8,128)(2,1)S(1)} %fusion.25) | copy-start | bytes 1966084
  84.4 8.9 %slice-start.1 = ((s8[4718592]{0:T(1024)(128)(4,1)}), s8[4194304]{0:T(1024)(128)(4,1)S(1)}, s32[]{:S(2)}) async-start(s8[4718592]{0:T(1024)(128)(4,1)} %bitcast.101), calls=%async_computation.1 | async-start | bytes 8388608
  84.6 8.8 %slice-start.2 = ((s8[4718592]{0:T(1024)(128)(4,1)}), s8[524288]{0:T(1024)(128)(4,1)S(1)}, s32[]{:S(2)}) async-start(s8[4718592]{0:T(1024)(128)(4,1)} %bitcast.101), calls=%async_computation.2 | async-start | bytes 1048576
  106.5 3.3 %slice-start = ((bf16[10,64,512]{2,1,0:T(8,128)(2,1)}), bf16[8,64,512]{2,1,0:T(8,128)(2,1)S(1)}, s32[]{:S(2)}) async-start(bf16[10,64,512]{2,1,0:T(8,128)(2,1)} %copy-done.1), calls=%async_computation | async-start | bytes 1048576 | tf_op jit(solution)/shard_map/slice | solution.py:30
  116.8 3.1 %copy-start = (f32[16,128,512]{2,1,0:T(8,128)S(1)}, f32[16,128,512]{2,1,0:T(8,128)}, u32[]{:S(2)}) copy-start(f32[16,128,512]{2,1,0:T(8,128)} %fusion.8) | copy-start | bytes 12582916
  116.8 3.1 %copy-start.4 = (f32[512]{0:T(512)S(1)}, f32[512]{0:T(512)}, u32[]{:S(2)}) copy-start(f32[512]{0:T(512)} %param.13) | copy-start | bytes 6148
